TPU v7x, 32 devices: a whole 2x2x4 slice. The times are simulated.
32 devices in a mesh: kern: 16 (over z, y, x), walk: 2 (over core).
Axes of the slice: x: 2, y: 2, z: 4, core: 2. Of those that a mesh axis runs over, the one named last changes fastest.
Arguments:
- walkers: float32 [8, 2048], P(None, 'walk'), may hold values from -5 to 5
- centers: float32 [8, 32768], P(None, 'kern'), may hold values from -5 to 5
- sigmas: float32 [8, 32768], P(None, 'kern'), may hold values from 0.6 to 1.5
- heights: float32 [32768], P('kern'), may hold values from 0.2 to 2
- kernel_live: int32 [16], P('kern'), may hold values from 512 to 2048, as said below
- merge_target: int32 [2048], P('walk'), may hold values from 0 to 32767, as said below
- new_sigma: float32 [8], replicated, may hold values from 0.2 to 0.6
- norm_old: float32 [1], replicated, may hold values from 0.003 to 0.03
Outputs:
- bias: float32 [2048], P('walk')
- force: float32 [8, 2048], P(None, 'walk')
- new_heights: float32 [32768], P('kern')
- new_centers: float32 [8, 32768], P(None, 'kern')
- new_sigmas: float32 [8, 32768], P(None, 'kern')
- log_norm: float32 [1], replicated
Inputs may be any that keep to these rules, and one draw needn't show every extreme that they name: `kernel_live`: slots from this number up are empty; some shard is full in every draw. `merge_target`: each entry is shard * 2048 + slot with slot below that shard's kernel_live; among the 1024 walkers of one index of walk at most 128 target one shard, every shard is targeted, and some shard receives exactly 128 in every block.
All inputs are finite; a program needn't handle non-finite values.
Results may differ from a plain program's by a relative error of at most 0.0003.
Values sent between devices are 32-bit elements; how exact they have to be, the bound alone decides.
A program may use at most 64 MiB of HBM per device.

v0:
```python
import jax
import jax.numpy as jnp
from jax import lax
from jax.sharding import PartitionSpec as P

PREFACTOR = 0.9
EPSILON = 0.01
RATE = 0.25


def compact(payload, local_target, shard_len, capacity):
    owned = (local_target >= 0) & (local_target < shard_len)
    position = jnp.cumsum(owned.astype(jnp.int32)) - 1
    table = (position[None, :] == jnp.arange(capacity, dtype=jnp.int32)[:, None]) & owned[None, :]
    packed = lax.dot_general(
        payload,
        table.astype(jnp.float32),
        (((1,), (1,)), ((), ())),
        precision=lax.Precision.HIGHEST,
    )
    filled = jnp.any(table, 1)
    slots = jnp.sum(jnp.where(table, local_target[None, :], 0), 1)
    return (packed, jnp.where(filled, slots, -1))


def per_device(walkers, centers, sigmas, heights, kernel_live, merge_target, new_sigma, norm_old):
    shard_len = centers.shape[1]
    walk_len = walkers.shape[1]
    kern_count = lax.axis_size("kern")
    walk_count = lax.axis_size("walk")
    shard_index = lax.axis_index("kern")
    capacity = 2 * walk_len // kern_count
    live_count = kernel_live[0]
    alive = (jnp.arange(shard_len, dtype=jnp.int32) < live_count).astype(jnp.float32)
    inverse_var = 1.0 / (sigmas * sigmas)
    kernel_feat = jnp.concatenate(
        [
            -0.5 * inverse_var,
            centers * inverse_var,
            (jnp.log(heights) - 0.5 * jnp.sum(centers * centers * inverse_var, 0))[None],
        ],
        0,
    )
    kernel_mom = jnp.concatenate(
        [alive[None], inverse_var * alive, centers * inverse_var * alive], 0
    )
    walker_feat = jnp.concatenate(
        [walkers * walkers, walkers, jnp.ones((1, walk_len), jnp.float32)], 0
    )
    block_len = 1024

    def step(running, block_index):
        start = block_index * block_len
        feat = lax.dynamic_slice_in_dim(kernel_feat, start, block_len, 1)
        moms = lax.dynamic_slice_in_dim(kernel_mom, start, block_len, 1)
        expo = lax.dot_general(
            feat, walker_feat, (((0,), (0,)), ((), ())), precision=lax.Precision.HIGHEST
        )
        return (running + jnp.dot(moms, jnp.exp(expo), precision=lax.Precision.HIGHEST), None)

    moments, _ = lax.scan(
        step,
        jnp.zeros((17, walk_len), jnp.float32),
        jnp.arange(shard_len // block_len, dtype=jnp.int32),
    )
    payload = jnp.concatenate([moments, jnp.full((1, walk_len), live_count.astype(jnp.float32))], 0)
    summed = lax.psum(payload, "kern")
    live_total = summed[17]
    density = summed[0] / live_total
    grad = (-walkers * summed[1:9] + summed[9:17]) / live_total
    norm_value = norm_old[0]
    ratio = density / norm_value + EPSILON
    bias = PREFACTOR * jnp.log(ratio)
    force = -PREFACTOR * grad / (norm_value * ratio)
    weight = jnp.exp(bias)
    density_sum = lax.psum(jnp.sum(density), "walk")
    log_norm = jnp.log((1.0 - RATE) * norm_old + RATE * density_sum / (walk_len * walk_count))
    new_rows = jnp.concatenate([walkers, weight[None]], 0)
    every_row = lax.all_gather(new_rows, "walk", axis=1, tiled=True)
    every_target = lax.all_gather(merge_target, "walk", axis=0, tiled=True)
    local_target = (every_target - shard_index * shard_len).reshape(walk_count, walk_len)
    packed, slots = jax.vmap(compact, in_axes=(1, 0, None, None))(
        every_row.reshape(9, walk_count, walk_len), local_target, shard_len, capacity
    )
    packed = packed.transpose(1, 0, 2).reshape(9, walk_count * capacity)
    slots = slots.reshape(-1)
    placing = (slots[:, None] == jnp.arange(shard_len, dtype=jnp.int32)[None, :]).astype(
        jnp.float32
    )
    target_center = lax.dot_general(
        centers, placing, (((1,), (1,)), ((), ())), precision=lax.Precision.HIGHEST
    )
    offset = packed[:8] - target_center
    new_weight = packed[8]
    feat = jnp.concatenate(
        [
            new_weight[None],
            new_weight * offset,
            new_weight * (offset * offset + (new_sigma * new_sigma)[:, None]),
        ],
        0,
    )
    merged_sums = jnp.dot(feat, placing, precision=lax.Precision.HIGHEST)
    new_heights = heights + merged_sums[0]
    delta = merged_sums[1:9] / new_heights
    new_centers = centers + delta
    new_sigmas = jnp.sqrt(
        (heights * sigmas * sigmas + merged_sums[9:17]) / new_heights - delta * delta
    )
    return (bias, force, new_heights, new_centers, new_sigmas, log_norm)


def solution(mesh):
    in_specs = (
        P(None, "walk"),
        P(None, "kern"),
        P(None, "kern"),
        P("kern"),
        P("kern"),
        P("walk"),
        P(),
        P(),
    )
    out_specs = (P("walk"), P(None, "walk"), P("kern"), P(None, "kern"), P(None, "kern"), P())
    return jax.shard_map(
        per_device, mesh=mesh, in_specs=in_specs, out_specs=out_specs, check_vma=False
    )
```

profile of v0, /device:TPU:0, one launch (start us, length us, event | category | flops | bytes accessed | tf_op | source)
XLA Modules:
  0.0 161.9 jit_solution(14939996878274551211)
XLA Ops:
  7.9 0.8 mul.126
  8.7 0.9 broadcast_multiply_fusion.1
  9.7 0.7 multiply_subtract_fusion
  10.4 0.8 maximum_maximum_fusion
  11.4 21.7 %while.11 = (s32[]{:T(128)}, f32[17,1024]{1,0:T(8,128)S(1)}, s32[2]{0:T(128)S(1)}, f32[17,2048]{1,0:T(8,128)S(1)}, f32[17,2048]{1,0:T(8,128)S(1)}, /*index=5*/f3...) while((s32[]{:T(128)}, f32[17,1024]{1,0:T(8,128)S(1)}, s32[2]{0:T(128)S(1)}, ...), condition=%wide.region_2.3_spmd.clone, body=%wide.region_1.2_spmd.clone.sunk | while | flops 427853824 | bytes 8851633 | solution.py:61
  11.4 0.6 dynamic_slice.22
  12.6 5.1 %fusion.53 = f32[1024,1024]{1,0:T(8,128)} fusion(f32[17,1024]{1,0:T(8,128)S(1)} %get-tuple-element.155, f32[17,2048]{1,0:T(8,128)S(1)} %get-tuple-element.154, s32[]{:T(128)S(6)} %select_n.26), kind=kOutput, calls=%fused_computation.3.clone.1 | convolution fusion | flops 213909504 | bytes 4390916 | tf_op jit(solution)/shard_map/while/body/eval_jaxpr/dot_general | solution.py:56
  17.7 4.5 %fusion.54 = f32[17,1024]{1,0:T(8,128)S(1)} fusion(f32[1024,1024]{1,0:T(8,128)} %fusion.53, f32[17,1024]{1,0:T(8,128)S(1)} %get-tuple-element.141, f32[17,2048]{1,0:T(8,128)S(1)} %get-tuple-element.153, s32[]{:T(128)S(6)} %select_n.26, pred[]{:T(512)S(6)} %compare.4), kind=kOutput, calls=%fused_computation.2.clone.1 | convolution fusion | flops 213944320 | bytes 4460549 | tf_op jit(solution)/shard_map/while/body/eval_jaxpr/dot_general | solution.py:59
  22.3 0.6 dynamic_slice.22
  23.5 5.1 %fusion.53 = f32[1024,1024]{1,0:T(8,128)} fusion(f32[17,1024]{1,0:T(8,128)S(1)} %get-tuple-element.155, f32[17,2048]{1,0:T(8,128)S(1)} %get-tuple-element.154, s32[]{:T(128)S(6)} %select_n.26), kind=kOutput, calls=%fused_computation.3.clone.1 | convolution fusion | flops 213909504 | bytes 4390916 | tf_op jit(solution)/shard_map/while/body/eval_jaxpr/dot_general | solution.py:56
  28.6 4.5 %fusion.54 = f32[17,1024]{1,0:T(8,128)S(1)} fusion(f32[1024,1024]{1,0:T(8,128)} %fusion.53, f32[17,1024]{1,0:T(8,128)S(1)} %get-tuple-element.141, f32[17,2048]{1,0:T(8,128)S(1)} %get-tuple-element.153, s32[]{:T(128)S(6)} %select_n.26, pred[]{:T(512)S(6)} %compare.4), kind=kOutput, calls=%fused_computation.2.clone.1 | convolution fusion | flops 213944320 | bytes 4460549 | tf_op jit(solution)/shard_map/while/body/eval_jaxpr/dot_general | solution.py:59
  33.1 0.6 concatenate.21
  33.8 2.0 %all_gather.7 = s32[2048]{0:T(1024)S(1)} all-gather(s32[1024]{0:T(1024)S(1)} %copy-done.5), channel_id=1, replica_groups=mesh['kern'=16,'walk'=2] {'walk'}, dimensions={0}, use_global_device_ids=true | all-gather | bytes 12288 | tf_op jit(solution)/shard_map/all_gather | solution.py:80
  35.8 0.6 reduce-window.6
  38.0 103.1 %all-reduce.3.cloned.1.call-done = f32[18,1024]{1,0:T(8,128)} async-done(((f32[18,1024]{1,0:T(8,128)}), f32[18,1024]{1,0:T(8,128)}) %all-reduce.3.cloned.1.call-update) | async-done | bytes 73744 | tf_op jit(solution)/shard_map/psum | solution.py:67
  141.2 0.8 multiply_exponential_fusion
  142.0 1.9 %all_gather.6 = f32[9,2048]{1,0:T(8,128)S(1)} all-gather(f32[9,1024]{1,0:T(8,128)S(1)} %pad_maximum_fusion.2), channel_id=1, replica_groups=mesh['kern'=16,'walk'=2] {'walk'}, dimensions={1}, use_global_device_ids=true | all-gather | bytes 110592 | tf_op jit(solution)/shard_map/all_gather | solution.py:79
  144.0 0.6 convolution_bitcast_fusion
  144.6 1.1 broadcast_multiply_fusion.3
  145.8 0.8 fusion.10
  146.6 0.7 fusion.25
  147.4 1.2 divide_reduce_fusion
  148.6 3.1 %psum.15 = f32[]{:T(128)} all-reduce(f32[]{:T(128)} %get-tuple-element.89), channel_id=1, replica_groups=mesh['kern'=16,'walk'=2] {'walk'}, use_global_device_ids=true, to_apply=%region_9.10 | all-reduce | flops 1 | bytes 8 | tf_op jit(solution)/shard_map/psum | solution.py:76
  152.4 1.6 fusion.28
  (39 shorter events, 1.4 us)
Async XLA Ops:
  7.2 134.0 %all-reduce.3.cloned.1.call-start = ((), (), s32[]{:S(2)}) async-start(), calls=%async_computation | async-start | bytes 196608 | tf_op jit(solution)/shard_map/psum | solution.py:67
  11.3 22.5 %copy-start.5 = (s32[1024]{0:T(1024)S(1)}, s32[1024]{0:T(1024)}, u32[]{:S(2)}) copy-start(s32[1024]{0:T(1024)} %param.15) | copy-start | bytes 12292
  11.3 26.7 %copy-start.6 = (f32[8]{0:T(128)S(1)}, f32[8]{0:T(128)}, u32[]{:S(2)}) copy-start(f32[8]{0:T(128)} %param.16) | copy-start | bytes 100
  11.3 130.7 %copy-start = (f32[8,1024]{1,0:T(8,128)S(1)}, f32[8,1024]{1,0:T(8,128)}, u32[]{:S(2)}) copy-start(f32[8,1024]{1,0:T(8,128)} %param.10) | copy-start | bytes 98308
  11.4 133.3 %copy-start.1 = (f32[8,2048]{1,0:T(8,128)S(1)}, f32[8,2048]{1,0:T(8,128)}, u32[]{:S(2)}) copy-start(f32[8,2048]{1,0:T(8,128)} %param.11) | copy-start | bytes 196612
  11.4 135.2 %copy-start.3 = (f32[2048]{0:T(1024)S(1)}, f32[2048]{0:T(1024)}, u32[]{:S(2)}) copy-start(f32[2048]{0:T(1024)} %param.13) | copy-start | bytes 24580
  11.4 135.2 %copy-start.2 = (f32[8,2048]{1,0:T(8,128)S(1)}, f32[8,2048]{1,0:T(8,128)}, u32[]{:S(2)}) copy-start(f32[8,2048]{1,0:T(8,128)} %param.12) | copy-start | bytes 196612
  146.6 7.3 %copy-start.4 = (f32[2048]{0:T(1024)}, f32[2048]{0:T(1024)S(1)}, u32[]{:S(2)}) copy-start(f32[2048]{0:T(1024)S(1)} %add.67) | copy-start | bytes 24580
Sparse Core Ops, SparseCore 0:
  33.9 107.2 all-reduce.2
where the time goes:
time: 163 us; the launch traced here: 162 us
  waiting for transfers between devices  103 us (63%)
  matrix products  21.7 us (13%)
  between operations  17.4 us (11%)
  other arithmetic  9.01 us (6%)
  blocking collectives  6.94 us (4%)
  local copies, waits for them, and re-layouts  2.25 us (1%)
    psum x1, waiting for transfers between devices, per_device(): summed = lax.psum(payload, 'kern')  103 us
    dot_general x2, matrix products, step(): lax.dot_general(feat, walker_feat, (((0,), (0,)), ((), ())), precision=la...  10.2 us
    dot_general x2, matrix products, step(): jnp.dot(moms, jnp.exp(expo), precision=lax.Precision.HIGHEST)  8.99 us
  transfers between devices with their start and end apart: 1, of which 1 were waited for; matrix products, arithmetic and copies ran while one was open for 1% of the time, Pallas kernels for 0%

commit v1 on v0

v1 whole, which is shorter than its diff:
```python
import functools
import math

import jax
import jax.numpy as jnp
from jax import lax
from jax.experimental import pallas as pl
from jax.experimental.pallas import tpu as pltpu
from jax.sharding import PartitionSpec as P

PREFACTOR = 0.9
EPSILON = 0.01
RATE = 0.25
LANES = 128
LOG2E = math.log2(math.e)
MESH = pl.DeviceIdType.MESH
F32 = jnp.float32
BF16 = jnp.bfloat16
VMEM = pl.BlockSpec(memory_space=pltpu.VMEM)
SMEM = pl.BlockSpec(memory_space=pltpu.SMEM)


def split(x):
    high = x.astype(BF16).astype(F32)
    rest = x - high
    middle = rest.astype(BF16).astype(F32)
    low = (rest - middle).astype(BF16).astype(F32)
    return high, middle, low


def sums_kernel(dims, groups, walkers_ref, centers_ref, sigmas_ref, heights_ref, live_ref,
                out_ref, own_ref, walker_feat, kernel_feat, kernel_mom, total):
    walk_len = walkers_ref.shape[1]
    shard_len = centers_ref.shape[1]
    per = dims // groups
    walkers = walkers_ref[...]
    sq_h, sq_m, sq_l = split(walkers * walkers)
    wk_h, wk_m, wk_l = split(walkers)
    h, m, l = [sq_h, wk_h], [sq_m, wk_m], [sq_l, wk_l]
    row = lax.broadcasted_iota(jnp.int32, (8, walk_len), 0)
    ones = jnp.where(row < 3, 1.0, 0.0).astype(F32)
    pad = jnp.zeros((LANES - 12 * dims - 8, walk_len), F32)
    stacked = jnp.concatenate(h + m + h + m + l + h + [ones, pad], 0)
    walker_feat[...] = stacked.T.astype(BF16)

    centers = centers_ref[...]
    sigmas = sigmas_ref[...]
    inverse_var = 1.0 / (sigmas * sigmas)
    scaled = centers * inverse_var
    constant = jnp.log(heights_ref[...]) - 0.5 * jnp.sum(centers * scaled, 0, keepdims=True)
    k_sq = split((-0.5 * LOG2E) * inverse_var)
    k_lin = split(LOG2E * scaled)
    k_con = split(LOG2E * constant)
    row = lax.broadcasted_iota(jnp.int32, (8, shard_len), 0)
    con = jnp.where(row == 0, k_con[0], jnp.where(row == 1, k_con[1], jnp.where(row == 2, k_con[2], 0.0)))
    h, m, l = [[k_sq[i], k_lin[i]] for i in range(3)]
    pad = jnp.zeros((LANES - 12 * dims - 8, shard_len), F32)
    kernel_feat[...] = jnp.concatenate(h + h + m + m + h + l + [con, pad], 0).astype(BF16)

    live = live_ref[0]
    alive = (lax.broadcasted_iota(jnp.int32, (8, shard_len), 1) < live).astype(F32)
    first = jnp.where(row == 0, alive, 0.0)
    mom_a = split(inverse_var * alive)
    mom_c = split(scaled * alive)
    pad = jnp.zeros((LANES - 6 * dims - 8, shard_len), F32)
    rows = [mom_a[0], mom_c[0], mom_a[1], mom_c[1], mom_a[2], mom_c[2], first, pad]
    kernel_mom[...] = jnp.concatenate(rows, 0).T.astype(BF16)

    block = 256
    for index in range(shard_len // block):
        part = slice(index * block, (index + 1) * block)
        expo = jnp.dot(walker_feat[...], kernel_feat[:, part], preferred_element_type=F32)
        e = jnp.exp2(expo)
        high = e.astype(BF16)
        low = (e - high.astype(F32)).astype(BF16)
        moms = kernel_mom[part, :]
        add = jnp.dot(high, moms, preferred_element_type=F32) + jnp.dot(
            low, moms, preferred_element_type=F32
        )
        if index == 0:
            total[...] = add
        else:
            total[...] += add

    moments = total[...].T
    a_sum = moments[0:dims] + moments[2 * dims : 3 * dims] + moments[4 * dims : 5 * dims]
    c_sum = moments[dims : 2 * dims] + moments[3 * dims : 4 * dims] + moments[5 * dims : 6 * dims]
    density = moments[6 * dims : 6 * dims + 1]
    live_row = jnp.full((1, LANES), live, jnp.int32).astype(F32)
    for chunk in range(walk_len // LANES):
        part = slice(chunk * LANES, (chunk + 1) * LANES)
        for group in range(groups):
            unit = chunk * groups + group
            rows = slice(group * per, (group + 1) * per)
            out_ref[unit, 0:per, :] = a_sum[rows, part]
            out_ref[unit, per : 2 * per, :] = c_sum[rows, part]
            out_ref[unit, 2 * per : 2 * per + 1, :] = density[:, part]
            out_ref[unit, 2 * per + 1 : 2 * per + 2, :] = live_row
            own_ref[unit] = walkers[rows, part]


def exchange_kernel(kern_count, walk_count, groups, sums_ref, own_ref, walkers_ref, target_ref, norm_ref,
                    share_ref, density_ref, all_walkers_ref, all_targets_ref,
                    got, mine, shared, far, far_walkers, far_targets,
                    send_a, recv_a, send_b, recv_b, send_c, recv_c, send_w, recv_w, send_t, recv_t):
    me = lax.axis_index("kern")
    walk = lax.axis_index("walk")
    per = own_ref.shape[1]
    chunks = kern_count // groups
    my_chunk = me // groups
    my_group = me % groups
    norm = norm_ref[0]

    def peer(step):
        return lax.rem(me + step, kern_count)

    def other(step):
        return lax.rem(walk + step, walk_count)

    def far_kern(index):
        return index * groups + my_group

    barrier = pltpu.get_barrier_semaphore()

    def greet(step, carry):
        pl.semaphore_signal(barrier, inc=1, device_id=(peer(step), walk), device_id_type=MESH)
        return carry

    lax.fori_loop(1, kern_count, greet, 0)
    for step in range(1, walk_count):
        def greet_far(index, carry):
            pl.semaphore_signal(
                barrier, inc=1, device_id=(far_kern(index), other(step)), device_id_type=MESH
            )
            return carry

        lax.fori_loop(0, chunks, greet_far, 0)
    pl.semaphore_wait(barrier, kern_count - 1 + (walk_count - 1) * chunks)

    def copy_a(target, source):
        return pltpu.make_async_remote_copy(
            src_ref=sums_ref.at[target], dst_ref=got.at[source],
            send_sem=send_a.at[target], recv_sem=recv_a.at[source],
            device_id=(target, walk), device_id_type=MESH,
        )

    def start_a(step, carry):
        copy_a(peer(step), me).start()
        return carry

    lax.fori_loop(1, kern_count, start_a, 0)

    def copy_w(step, source):
        return (
            pltpu.make_async_remote_copy(
                src_ref=walkers_ref, dst_ref=far_walkers.at[source],
                send_sem=send_w.at[step], recv_sem=recv_w.at[source],
                device_id=(me, other(step)), device_id_type=MESH,
            ),
            pltpu.make_async_remote_copy(
                src_ref=target_ref, dst_ref=far_targets.at[source],
                send_sem=send_t.at[step], recv_sem=recv_t.at[source],
                device_id=(me, other(step)), device_id_type=MESH,
            ),
        )

    for step in range(1, walk_count):
        for copy in copy_w(step, walk):
            copy.start()

    got[me] = sums_ref[me]
    far_walkers[walk] = walkers_ref[...]
    far_targets[walk] = target_ref[...]

    def wait_a(step, carry):
        copy_a(peer(step), peer(step)).wait_recv()
        return carry

    lax.fori_loop(1, kern_count, wait_a, 0)
    total = got[0]
    for source in range(1, kern_count):
        total = total + got[source]

    live_total = total[2 * per + 1 : 2 * per + 2]
    density = total[2 * per : 2 * per + 1] / live_total
    grad = (-own_ref[me] * total[0:per] + total[per : 2 * per]) / live_total
    ratio = density / norm + EPSILON
    force = -PREFACTOR * grad / (norm * ratio)
    mine[0:1, :] = density
    mine[1 : per + 1, :] = force
    shared[me, 0:1, :] = density
    shared[me, 1 : per + 1, :] = force

    def copy_b(target, source):
        return pltpu.make_async_remote_copy(
            src_ref=mine, dst_ref=shared.at[source],
            send_sem=send_b.at[target], recv_sem=recv_b.at[source],
            device_id=(target, walk), device_id_type=MESH,
        )

    def copy_c(step, index, chunk, source):
        return pltpu.make_async_remote_copy(
            src_ref=mine, dst_ref=far.at[source, chunk],
            send_sem=send_c.at[step, index], recv_sem=recv_c.at[source, chunk],
            device_id=(far_kern(index), other(step)), device_id_type=MESH,
        )

    for step in range(1, walk_count):
        def start_c(index, carry):
            copy_c(step, index, my_chunk, walk).start()
            return carry

        lax.fori_loop(0, chunks, start_c, 0)

    def start_b(step, carry):
        copy_b(peer(step), me).start()
        return carry

    lax.fori_loop(1, kern_count, start_b, 0)

    def wait_b(step, carry):
        copy_b(peer(step), peer(step)).wait_recv()
        return carry

    lax.fori_loop(1, kern_count, wait_b, 0)
    for chunk in range(chunks):
        far[walk, chunk] = shared[chunk * groups]
    share_ref[...] = shared[...]
    for step in range(1, walk_count):
        def wait_c(index, carry):
            copy_c(step, index, index, other(step)).wait_recv()
            return carry

        lax.fori_loop(0, chunks, wait_c, 0)
        for copy in copy_w(step, other(step)):
            copy.wait_recv()
    for block in range(walk_count):
        for chunk in range(chunks):
            density_ref[block, :, chunk * LANES : (chunk + 1) * LANES] = far[block, chunk][0:1, :]
    all_walkers_ref[...] = far_walkers[...]
    all_targets_ref[...] = far_targets[...]

    def wait_sends(step, carry):
        copy_a(peer(step), me).wait_send()
        copy_b(peer(step), me).wait_send()
        return carry

    lax.fori_loop(1, kern_count, wait_sends, 0)
    for step in range(1, walk_count):
        def wait_send_c(index, carry):
            copy_c(step, index, my_chunk, walk).wait_send()
            return carry

        lax.fori_loop(0, chunks, wait_send_c, 0)
        for copy in copy_w(step, walk):
            copy.wait_send()


def merge_kernel(groups, share_ref, density_ref, walkers_ref, targets_ref, centers_ref, sigmas_ref, heights_ref,
                 new_sigma_ref, norm_ref,
                 bias_ref, force_ref, new_heights_ref, new_centers_ref, new_sigmas_ref, log_norm_ref,
                 merged):
    dims, shard_len = centers_ref.shape
    walk_count, _, walk_len = density_ref.shape
    per = dims // groups
    chunks = walk_len // LANES
    norm = norm_ref[0]

    def biased(density):
        return PREFACTOR * jnp.log(density / norm + EPSILON)

    for chunk in range(chunks):
        part = slice(chunk * LANES, (chunk + 1) * LANES)
        bias_ref[:, part] = biased(share_ref[chunk * groups][0:1, :])
        for group in range(groups):
            force_ref[group * per : (group + 1) * per, part] = share_ref[chunk * groups + group][1 : per + 1, :]

    density_sum = jnp.zeros((1, 1), F32)
    for block in range(walk_count):
        density_sum = density_sum + jnp.sum(density_ref[block], 1, keepdims=True)
    log_norm_ref[...] = jnp.log((1.0 - RATE) * norm + RATE * density_sum / (walk_len * walk_count))

    base = lax.axis_index("kern") * shard_len
    row = lax.broadcasted_iota(jnp.int32, (8, walk_len), 0)
    tile = 256
    for block in range(walk_count):
        weight = jnp.exp(biased(density_ref[block]))
        walkers = walkers_ref[block]
        lin = split(weight * walkers)
        sq = split(weight * (walkers * walkers))
        plain = split(weight)
        last = jnp.where(row == 0, plain[0], jnp.where(row == 1, plain[1], jnp.where(row == 2, plain[2], 0.0)))
        pad = jnp.zeros((8, walk_len), F32)
        feat = jnp.concatenate(
            [lin[0], sq[0], lin[1], sq[1], lin[2], sq[2], last, pad], 0
        ).astype(BF16)
        local = targets_ref[block] - base
        for index in range(shard_len // tile):
            slot = lax.broadcasted_iota(jnp.int32, (tile, walk_len), 0) + index * tile
            placing = jnp.where(slot == local, 1.0, 0.0).astype(BF16)
            add = lax.dot_general(
                feat, placing, (((1,), (1,)), ((), ())), preferred_element_type=F32
            )
            part = slice(index * tile, (index + 1) * tile)
            if block == 0:
                merged[:, part] = add
            else:
                merged[:, part] += add

    sums = merged[...]
    first = sums[0:dims] + (sums[2 * dims : 3 * dims] + sums[4 * dims : 5 * dims])
    second = sums[dims : 2 * dims] + (sums[3 * dims : 4 * dims] + sums[5 * dims : 6 * dims])
    at = 6 * dims
    gain = sums[at : at + 1] + (sums[at + 1 : at + 2] + sums[at + 2 : at + 3])
    dim = lax.broadcasted_iota(jnp.int32, (dims, 1), 0)
    new_sigma = jnp.zeros((dims, 1), F32)
    for d in range(dims):
        new_sigma = jnp.where(dim == d, new_sigma_ref[d], new_sigma)
    centers = centers_ref[...]
    sigmas = sigmas_ref[...]
    heights = heights_ref[...]
    shift = first - centers * gain
    spread = second - 2.0 * centers * first + centers * centers * gain + new_sigma * new_sigma * gain
    new_heights = heights + gain
    delta = shift / new_heights
    new_heights_ref[...] = new_heights
    new_centers_ref[...] = centers + delta
    new_sigmas_ref[...] = jnp.sqrt((heights * sigmas * sigmas + spread) / new_heights - delta * delta)


def per_device(walkers, centers, sigmas, heights, kernel_live, merge_target, new_sigma, norm_old):
    dims, walk_len = walkers.shape
    shard_len = centers.shape[1]
    kern_count = lax.axis_size("kern")
    walk_count = lax.axis_size("walk")
    chunks = walk_len // LANES
    groups = kern_count // chunks
    per = dims // groups
    height_row = heights.reshape(1, shard_len)

    sums, own = pl.pallas_call(
        functools.partial(sums_kernel, dims, groups),
        out_shape=(
            jax.ShapeDtypeStruct((kern_count, 2 * per + 2, LANES), F32),
            jax.ShapeDtypeStruct((kern_count, per, LANES), F32),
        ),
        in_specs=[VMEM, VMEM, VMEM, VMEM, SMEM],
        out_specs=(VMEM, VMEM),
        scratch_shapes=[
            pltpu.VMEM((walk_len, LANES), BF16),
            pltpu.VMEM((LANES, shard_len), BF16),
            pltpu.VMEM((shard_len, LANES), BF16),
            pltpu.VMEM((walk_len, LANES), F32),
        ],
        name="sums",
    )(walkers, centers, sigmas, height_row, kernel_live)

    dma = pltpu.SemaphoreType.DMA
    share, density, all_walkers, all_targets = pl.pallas_call(
        functools.partial(exchange_kernel, kern_count, walk_count, groups),
        out_shape=(
            jax.ShapeDtypeStruct((kern_count, per + 1, LANES), F32),
            jax.ShapeDtypeStruct((walk_count, 1, walk_len), F32),
            jax.ShapeDtypeStruct((walk_count, dims, walk_len), F32),
            jax.ShapeDtypeStruct((walk_count, 1, walk_len), jnp.int32),
        ),
        in_specs=[VMEM, VMEM, VMEM, VMEM, SMEM],
        out_specs=(VMEM, VMEM, VMEM, VMEM),
        scratch_shapes=[
            pltpu.VMEM((kern_count, 2 * per + 2, LANES), F32),
            pltpu.VMEM((per + 1, LANES), F32),
            pltpu.VMEM((kern_count, per + 1, LANES), F32),
            pltpu.VMEM((walk_count, chunks, per + 1, LANES), F32),
            pltpu.VMEM((walk_count, dims, walk_len), F32),
            pltpu.VMEM((walk_count, 1, walk_len), jnp.int32),
            dma((kern_count,)), dma((kern_count,)),
            dma((kern_count,)), dma((kern_count,)),
            dma((walk_count, chunks)), dma((walk_count, chunks)),
            dma((walk_count,)), dma((walk_count,)),
            dma((walk_count,)), dma((walk_count,)),
        ],
        compiler_params=pltpu.CompilerParams(collective_id=0, has_side_effects=True),
        name="exchange",
    )(sums, own, walkers, merge_target.reshape(1, walk_len), norm_old)

    bias, force, new_heights, new_centers, new_sigmas, log_norm = pl.pallas_call(
        functools.partial(merge_kernel, groups),
        out_shape=(
            jax.ShapeDtypeStruct((1, walk_len), F32),
            jax.ShapeDtypeStruct((dims, walk_len), F32),
            jax.ShapeDtypeStruct((1, shard_len), F32),
            jax.ShapeDtypeStruct((dims, shard_len), F32),
            jax.ShapeDtypeStruct((dims, shard_len), F32),
            jax.ShapeDtypeStruct((1, 1), F32),
        ),
        in_specs=[VMEM] * 7 + [SMEM, SMEM],
        out_specs=(VMEM,) * 6,
        scratch_shapes=[pltpu.VMEM((6 * dims + 16, shard_len), F32)],
        name="merge",
    )(share, density, all_walkers, all_targets, centers, sigmas, height_row, new_sigma, norm_old)
    return (bias.reshape(walk_len), force, new_heights.reshape(shard_len), new_centers, new_sigmas, log_norm.reshape(1))


def solution(mesh):
    in_specs = (
        P(None, "walk"),
        P(None, "kern"),
        P(None, "kern"),
        P("kern"),
        P("kern"),
        P("walk"),
        P(),
        P(),
    )
    out_specs = (P("walk"), P(None, "walk"), P("kern"), P(None, "kern"), P(None, "kern"), P())
    return jax.shard_map(
        per_device, mesh=mesh, in_specs=in_specs, out_specs=out_specs, check_vma=False
    )
```

time: 163 us -> 32.7 us (0.20)
  waiting for transfers between devices: 103 us -> 0 us
  Pallas kernels: 0 us -> 30.5 us
  matrix products: 21.7 us -> 0 us
  between operations: 17.4 us -> 1.93 us
  other arithmetic: 9.01 us -> 0 us
  blocking collectives: 6.94 us -> 0 us
  local copies, waits for them, and re-layouts: 2.25 us -> 0 us
    psum x1 -> x0, waiting for transfers between devices: 103 us -> none  [per_device(): summed = lax.psum(payload, 'kern')]
    pallas_call x0 -> x3, Pallas kernels: none -> 30.5 us  [the longest x1 19.4 us: per_device(): pl.pallas_call(functools.partial(exchange_kernel, kern_count, walk_count,...]
    dot_general x7 -> x0, matrix products: 21.7 us -> none  [the longest x2 10.2 us: step(): lax.dot_general(feat, walker_feat, (((0,), (0,)), ((), ())), precision=la...]
    all_gather x2 -> x0, blocking collectives: 3.86 us -> none  [the longest x1 1.96 us: per_device(): every_target = lax.all_gather(merge_target, 'walk', axis=0, tiled=True)]
    psum x1 -> x0, blocking collectives: 3.08 us -> none  [per_device(): density_sum = lax.psum(jnp.sum(density), 'walk')]
    mul x4 -> x0, other arithmetic: 1.76 us -> none  [the longest x1 0.91 us: per_device(): centers * inverse_var * alive]
  transfers between devices with their start and end apart: 1 -> 0, of which waited for: 1 -> 0; matrix products, arithmetic and copies ran while one was open for 1% -> 0% of each run, Pallas kernels for 0% -> 0%
where the time goes in v1:
time: 32.7 us; the launch traced here: 32.4 us
  Pallas kernels  30.5 us (93%)
  between operations  1.93 us (6%)
    pallas_call x1, Pallas kernels, per_device(): pl.pallas_call(functools.partial(exchange_kernel, kern_count, walk_count,...  19.4 us
    pallas_call x1, Pallas kernels, per_device(): pl.pallas_call(functools.partial(sums_kernel, dims, groups), out_shape=(j...  6.9 us
    pallas_call x1, Pallas kernels, per_device(): pl.pallas_call(functools.partial(merge_kernel, groups), out_shape=(jax.Sh...  4.22 us

profile of v1, /device:TPU:0, one launch (start us, length us, event | category | flops | bytes accessed | tf_op | source)
XLA Modules:
  0.0 32.4 jit_solution(17727557639386859331)
XLA Ops:
  1.9 6.9 %sums.1 = (f32[16,10,128]{2,1,0:T(8,128)}, f32[16,4,128]{2,1,0:T(4,128)}) custom-call(f32[8,1024]{1,0:T(8,128)} %walkers_ref.3, f32[8,2048]{1,0:T(8,128)} %centers_ref.3, f32[8,2048]{1,0:T(8,128)} %sigmas_ref.3, f32[1,2048]{1,0:T(1,128)} %bitcast.5, s32[1]{0:T(128)S(6)} %copy.14.live_ref), custom_call_target="tpu_custom_call" | custom-call | tf_op jit(solution)/shard_map/sums/pallas_call | solution.py:341
  8.8 19.4 %exchange.1 = (f32[16,5,128]{2,1,0:T(8,128)}, f32[2,1,1024]{2,1,0:T(1,128)}, f32[2,8,1024]{2,1,0:T(8,128)}, s32[2,1,1024]{2,1,0:T(1,128)}) custom-call(f32[16,10,128]{2,1,0:T(8,128)} %get-tuple-element.18.sums_ref, f32[16,4,128]{2,1,0:T(4,128)} %get-tuple-element.19.own_ref, f32[8,1024]{1,0:T(8,128)} %walkers_ref.3, s32[1,1024]{1,0:T(1,128)} %bitcast.7, ...), custom_call_target="tpu_custom_call" | custom-call | tf_op jit(solution)/shard_map/exchange/pallas_call | solution.py:359
  28.2 4.2 %merge.1 = (f32[1,1024]{1,0:T(1,128)}, f32[8,1024]{1,0:T(8,128)}, f32[1,2048]{1,0:T(1,128)}, f32[8,2048]{1,0:T(8,128)}, f32[8,2048]{1,0:T(8,128)}, /*index=5*/f32[1,1]{1,0:T(1,128)}) custom-call(f32[16,5,128]{2,1,0:T(8,128)} %get-tuple-element.20.share_ref, f32[2,1,1024]{2,1,0:T(1,128)} %get-tuple-element.21.density_ref, ...), custom_call_target="tpu_custom_call" | custom-call | tf_op jit(solution)/shard_map/merge/pallas_call | solution.py:386

commit v2 on v1

v2 whole, which is shorter than its diff:
```python
import functools
import math

import jax
import jax.numpy as jnp
from jax import lax
from jax.experimental import pallas as pl
from jax.experimental.pallas import tpu as pltpu
from jax.sharding import PartitionSpec as P

PREFACTOR = 0.9
EPSILON = 0.01
RATE = 0.25
LANES = 128
LOG2E = math.log2(math.e)
MESH = pl.DeviceIdType.MESH
F32 = jnp.float32
BF16 = jnp.bfloat16
VMEM = pl.BlockSpec(memory_space=pltpu.VMEM)
SMEM = pl.BlockSpec(memory_space=pltpu.SMEM)


def split(x):
    high = x.astype(BF16).astype(F32)
    rest = x - high
    middle = rest.astype(BF16).astype(F32)
    low = (rest - middle).astype(BF16).astype(F32)
    return high, middle, low


def row_of(parts, width):
    row = lax.broadcasted_iota(jnp.int32, (8, width), 0)
    block = jnp.zeros((8, width), F32)
    for index, part in enumerate(parts):
        block = jnp.where(row == index, part, block)
    return block


def farthest_first(count):
    return sorted(range(count), key=lambda step: -min(step, count - step))


def sums_kernel(kern_count, walk_count, groups, capacity,
                walkers_ref, target_ref, centers_ref, sigmas_ref, heights_ref, live_ref, norm_ref,
                share_ref, density_ref, packed_ref, packed_slot_ref, packed_density_ref,
                walker_feat, kernel_feat, kernel_mom, sums, own, got, mine, shared, far,
                far_walkers, far_targets, table,
                send_a, recv_a, send_b, recv_b, send_c, recv_c, send_w, recv_w, send_t, recv_t):
    dims, walk_len = walkers_ref.shape
    shard_len = centers_ref.shape[1]
    per = dims // groups
    chunks = kern_count // groups
    me = lax.axis_index("kern")
    walk = lax.axis_index("walk")
    my_chunk = me // groups
    my_group = lax.rem(me, groups)
    norm = norm_ref[0]

    def peer(step):
        return lax.rem(me + step, kern_count)

    def other(step):
        return lax.rem(walk + step, walk_count)

    def far_kern(index):
        return index * groups + my_group

    barrier = pltpu.get_barrier_semaphore()

    def greet(step, carry):
        pl.semaphore_signal(barrier, inc=1, device_id=(peer(step), walk), device_id_type=MESH)
        return carry

    lax.fori_loop(1, kern_count, greet, 0)
    for step in range(1, walk_count):
        def greet_far(index, carry):
            pl.semaphore_signal(
                barrier, inc=1, device_id=(far_kern(index), other(step)), device_id_type=MESH
            )
            return carry

        lax.fori_loop(0, chunks, greet_far, 0)

    walkers = walkers_ref[...]
    sq_h, sq_m, sq_l = split(walkers * walkers)
    wk_h, wk_m, wk_l = split(walkers)
    h, m, l = [sq_h, wk_h], [sq_m, wk_m], [sq_l, wk_l]
    one = jnp.ones((1, walk_len), F32)
    pad = jnp.zeros((LANES - 12 * dims - 8, walk_len), F32)
    stacked = jnp.concatenate(h + m + h + m + l + h + [row_of([one] * 3, walk_len), pad], 0)
    walker_feat[...] = stacked.T.astype(BF16)

    centers = centers_ref[...]
    sigmas = sigmas_ref[...]
    inverse_var = 1.0 / (sigmas * sigmas)
    scaled = centers * inverse_var
    constant = jnp.log(heights_ref[...]) - 0.5 * jnp.sum(centers * scaled, 0, keepdims=True)
    k_sq = split((-0.5 * LOG2E) * inverse_var)
    k_lin = split(LOG2E * scaled)
    con = row_of(split(LOG2E * constant), shard_len)
    h, m, l = [[k_sq[i], k_lin[i]] for i in range(3)]
    pad = jnp.zeros((LANES - 12 * dims - 8, shard_len), F32)
    kernel_feat[...] = jnp.concatenate(h + h + m + m + h + l + [con, pad], 0).astype(BF16)

    live = live_ref[0]
    alive = (lax.broadcasted_iota(jnp.int32, (8, shard_len), 1) < live).astype(F32)
    mom_a = split(inverse_var * alive)
    mom_c = split(scaled * alive)
    pad = jnp.zeros((LANES - 6 * dims - 8, shard_len), F32)
    rows = [mom_a[0], mom_c[0], mom_a[1], mom_c[1], mom_a[2], mom_c[2], row_of([alive], shard_len), pad]
    kernel_mom[...] = jnp.concatenate(rows, 0).T.astype(BF16)

    live_row = jnp.full((1, LANES), live, jnp.int32).astype(F32)
    for unit in range(kern_count):
        chunk, group = unit // groups, unit % groups
        own[unit] = walkers[group * per : (group + 1) * per, chunk * LANES : (chunk + 1) * LANES]

    width = 2 * LANES
    quarters = walk_len // width
    units = kern_count // quarters
    block = min(512, shard_len)

    def copy_a(target, source):
        return pltpu.make_async_remote_copy(
            src_ref=sums.at[target], dst_ref=got.at[source],
            send_sem=send_a.at[target], recv_sem=recv_a.at[source],
            device_id=(target, walk), device_id_type=MESH,
        )

    def compute(step):
        quarter = lax.rem(me // units + step, quarters)
        feat = walker_feat[pl.ds(pl.multiple_of(quarter * width, width), width), :]
        total = None
        for index in range(shard_len // block):
            part = slice(index * block, (index + 1) * block)
            e = jnp.exp2(jnp.dot(feat, kernel_feat[:, part], preferred_element_type=F32))
            high = e.astype(BF16)
            low = (e - high.astype(F32)).astype(BF16)
            moms = kernel_mom[part, :]
            add = jnp.dot(high, moms, preferred_element_type=F32) + jnp.dot(
                low, moms, preferred_element_type=F32
            )
            total = add if total is None else total + add
        moments = total.T
        a_sum = moments[0:dims] + moments[2 * dims : 3 * dims] + moments[4 * dims : 5 * dims]
        c_sum = moments[dims : 2 * dims] + moments[3 * dims : 4 * dims] + moments[5 * dims : 6 * dims]
        density = moments[6 * dims : 6 * dims + 1]
        for chunk in range(2):
            part = slice(chunk * LANES, (chunk + 1) * LANES)
            for group in range(groups):
                unit = quarter * units + chunk * groups + group
                rows = slice(group * per, (group + 1) * per)
                sums[unit, 0:per, :] = a_sum[rows, part]
                sums[unit, per : 2 * per, :] = c_sum[rows, part]
                sums[unit, 2 * per : 2 * per + 1, :] = density[:, part]
                sums[unit, 2 * per + 1 : 2 * per + 2, :] = live_row

    def send(step):
        quarter = lax.rem(me // units + step, quarters)

        def start_a(index, carry):
            copy_a(quarter * units + lax.rem(me + index, units), me).start()
            return carry

        lax.fori_loop(0 if step else 1, units, start_a, 0)

    def copy_w(step, source):
        return (
            pltpu.make_async_remote_copy(
                src_ref=walkers_ref, dst_ref=far_walkers.at[source],
                send_sem=send_w.at[step], recv_sem=recv_w.at[source],
                device_id=(me, other(step)), device_id_type=MESH,
            ),
            pltpu.make_async_remote_copy(
                src_ref=target_ref, dst_ref=far_targets.at[source],
                send_sem=send_t.at[step], recv_sem=recv_t.at[source],
                device_id=(me, other(step)), device_id_type=MESH,
            ),
        )

    order = farthest_first(quarters)
    for position, step in enumerate(order):
        compute(step)
        if position == 1:
            pl.semaphore_wait(barrier, kern_count - 1 + (walk_count - 1) * chunks)
            send(order[0])
            for far_step in range(1, walk_count):
                for copy in copy_w(far_step, walk):
                    copy.start()
        if position >= 1:
            send(step)

    got[me] = sums[me]
    far_walkers[walk] = walkers
    far_targets[walk] = target_ref[...]
    for step in range(1, walk_count):
        for copy in copy_w(step, other(step)):
            copy.wait_recv()
    targets = [far_targets[index] for index in range(walk_count)]
    if walk_count % 8:
        targets.append(jnp.full((8 - walk_count % 8, walk_len), -1, jnp.int32))
    local = jnp.concatenate(targets, 0) - me * shard_len
    owned = (local >= 0) & (local < shard_len)
    before = lax.broadcasted_iota(jnp.int32, (walk_len, walk_len), 0) < lax.broadcasted_iota(
        jnp.int32, (walk_len, walk_len), 1
    )
    place = jnp.dot(
        jnp.where(owned, 1.0, 0.0).astype(BF16),
        jnp.where(before, 1.0, 0.0).astype(BF16),
        preferred_element_type=F32,
    )
    place = jnp.where(owned, place, -1.0)
    slot = jnp.where(owned, (local + 1).astype(F32), 0.0)
    want = lax.broadcasted_iota(jnp.int32, (capacity, walk_len), 0).astype(F32)

    def pack(feat, index):
        return lax.dot_general(
            feat.astype(BF16), table[index], (((1,), (1,)), ((), ())), preferred_element_type=F32
        )

    for index in range(walk_count):
        table[index] = jnp.where(want == place[index : index + 1], 1.0, 0.0).astype(BF16)
        high, middle, low = split(far_walkers[index])
        slot_rows = row_of(split(slot[index : index + 1]), walk_len)
        packed = pack(jnp.concatenate([high, middle, low, slot_rows], 0), index)
        packed_ref[index] = packed[0:dims] + (packed[dims : 2 * dims] + packed[2 * dims : 3 * dims])
        at = 3 * dims
        packed_slot_ref[index] = packed[at : at + 1] + packed[at + 1 : at + 2] + packed[at + 2 : at + 3] - 1.0

    def wait_a(step, carry):
        copy_a(peer(step), peer(step)).wait_recv()
        return carry

    lax.fori_loop(1, kern_count, wait_a, 0)
    total = got[0]
    for source in range(1, kern_count):
        total = total + got[source]

    live_total = total[2 * per + 1 : 2 * per + 2]
    density = total[2 * per : 2 * per + 1] / live_total
    grad = (-own[me] * total[0:per] + total[per : 2 * per]) / live_total
    ratio = density / norm + EPSILON
    force = -PREFACTOR * grad / (norm * ratio)
    mine[0:1, :] = density
    mine[1 : per + 1, :] = force

    def copy_b(target, source):
        return pltpu.make_async_remote_copy(
            src_ref=mine, dst_ref=shared.at[source],
            send_sem=send_b.at[target], recv_sem=recv_b.at[source],
            device_id=(target, walk), device_id_type=MESH,
        )

    def copy_c(step, index, chunk, source):
        return pltpu.make_async_remote_copy(
            src_ref=mine, dst_ref=far.at[source, chunk],
            send_sem=send_c.at[step, index], recv_sem=recv_c.at[source, chunk],
            device_id=(far_kern(index), other(step)), device_id_type=MESH,
        )

    def start_b(step, carry):
        copy_b(peer(step), me).start()
        return carry

    for step in range(1, walk_count):
        def start_c(index, carry):
            copy_c(step, lax.rem(my_chunk + index, chunks), my_chunk, walk).start()
            return carry

        half = chunks // 2
        lax.fori_loop(half, chunks, start_c, 0)
        lax.fori_loop(0, half, start_c, 0)
    lax.fori_loop(kern_count // 2, kern_count, start_b, 0)
    lax.fori_loop(1, kern_count // 2, start_b, 0)

    shared[me, 0:1, :] = density
    shared[me, 1 : per + 1, :] = force

    def wait_b(step, carry):
        copy_b(peer(step), peer(step)).wait_recv()
        return carry

    lax.fori_loop(1, kern_count, wait_b, 0)
    for chunk in range(chunks):
        far[walk, chunk] = shared[chunk * groups]
    share_ref[...] = shared[...]
    for step in range(1, walk_count):
        def wait_c(index, carry):
            copy_c(step, index, index, other(step)).wait_recv()
            return carry

        lax.fori_loop(0, chunks, wait_c, 0)
    for index in range(walk_count):
        whole = jnp.concatenate([far[index, chunk][0:1, :] for chunk in range(chunks)], 1)
        density_ref[index] = whole
        packed = pack(row_of(split(whole), walk_len), index)
        packed_density_ref[index] = packed[0:1] + packed[1:2] + packed[2:3]

    def wait_sends(step, carry):
        copy_a(peer(step), me).wait_send()
        copy_b(peer(step), me).wait_send()
        return carry

    lax.fori_loop(1, kern_count, wait_sends, 0)
    for step in range(1, walk_count):
        def wait_send_c(index, carry):
            copy_c(step, index, my_chunk, walk).wait_send()
            return carry

        lax.fori_loop(0, chunks, wait_send_c, 0)
        for copy in copy_w(step, walk):
            copy.wait_send()


def merge_kernel(groups, share_ref, density_ref, packed_ref, packed_slot_ref, packed_density_ref,
                 centers_ref, sigmas_ref, heights_ref, new_sigma_ref, norm_ref,
                 bias_ref, force_ref, new_heights_ref, new_centers_ref, new_sigmas_ref, log_norm_ref):
    dims, shard_len = centers_ref.shape
    walk_count, _, walk_len = density_ref.shape
    capacity = packed_ref.shape[2]
    per = dims // groups
    chunks = walk_len // LANES
    norm = norm_ref[0]

    def biased(density):
        return PREFACTOR * jnp.log(density / norm + EPSILON)

    for chunk in range(chunks):
        part = slice(chunk * LANES, (chunk + 1) * LANES)
        bias_ref[:, part] = biased(share_ref[chunk * groups][0:1, :])
        for group in range(groups):
            force_ref[group * per : (group + 1) * per, part] = share_ref[chunk * groups + group][1 : per + 1, :]

    density_sum = jnp.zeros((1, 1), F32)
    for index in range(walk_count):
        density_sum = density_sum + jnp.sum(density_ref[index], 1, keepdims=True)
    log_norm_ref[...] = jnp.log((1.0 - RATE) * norm + RATE * density_sum / (walk_len * walk_count))

    slots = lax.broadcasted_iota(jnp.int32, (shard_len, capacity), 0).astype(F32)
    sums = None
    for index in range(walk_count):
        weight = jnp.exp(biased(packed_density_ref[index]))
        walkers = packed_ref[index]
        lin = split(weight * walkers)
        sq = split(weight * (walkers * walkers))
        last = row_of(split(weight), capacity)
        pad = jnp.zeros((8, capacity), F32)
        feat = jnp.concatenate([lin[0], sq[0], lin[1], sq[1], lin[2], sq[2], last, pad], 0).astype(BF16)
        placing = jnp.where(slots == packed_slot_ref[index], 1.0, 0.0).astype(BF16)
        add = lax.dot_general(feat, placing, (((1,), (1,)), ((), ())), preferred_element_type=F32)
        sums = add if sums is None else sums + add

    first = sums[0:dims] + (sums[2 * dims : 3 * dims] + sums[4 * dims : 5 * dims])
    second = sums[dims : 2 * dims] + (sums[3 * dims : 4 * dims] + sums[5 * dims : 6 * dims])
    at = 6 * dims
    gain = sums[at : at + 1] + (sums[at + 1 : at + 2] + sums[at + 2 : at + 3])
    dim = lax.broadcasted_iota(jnp.int32, (dims, 1), 0)
    new_sigma = jnp.zeros((dims, 1), F32)
    for d in range(dims):
        new_sigma = jnp.where(dim == d, new_sigma_ref[d], new_sigma)
    centers = centers_ref[...]
    sigmas = sigmas_ref[...]
    heights = heights_ref[...]
    shift = first - centers * gain
    spread = second - 2.0 * centers * first + centers * centers * gain + new_sigma * new_sigma * gain
    new_heights = heights + gain
    delta = shift / new_heights
    new_heights_ref[...] = new_heights
    new_centers_ref[...] = centers + delta
    new_sigmas_ref[...] = jnp.sqrt((heights * sigmas * sigmas + spread) / new_heights - delta * delta)


def per_device(walkers, centers, sigmas, heights, kernel_live, merge_target, new_sigma, norm_old):
    dims, walk_len = walkers.shape
    shard_len = centers.shape[1]
    kern_count = lax.axis_size("kern")
    walk_count = lax.axis_size("walk")
    chunks = walk_len // LANES
    groups = kern_count // chunks
    per = dims // groups
    capacity = 2 * walk_len // kern_count
    height_row = heights.reshape(1, shard_len)

    dma = pltpu.SemaphoreType.DMA
    share, density, packed, packed_slot, packed_density = pl.pallas_call(
        functools.partial(sums_kernel, kern_count, walk_count, groups, capacity),
        out_shape=(
            jax.ShapeDtypeStruct((kern_count, per + 1, LANES), F32),
            jax.ShapeDtypeStruct((walk_count, 1, walk_len), F32),
            jax.ShapeDtypeStruct((walk_count, dims, capacity), F32),
            jax.ShapeDtypeStruct((walk_count, 1, capacity), F32),
            jax.ShapeDtypeStruct((walk_count, 1, capacity), F32),
        ),
        in_specs=[VMEM] * 5 + [SMEM, SMEM],
        out_specs=(VMEM,) * 5,
        scratch_shapes=[
            pltpu.VMEM((walk_len, LANES), BF16),
            pltpu.VMEM((LANES, shard_len), BF16),
            pltpu.VMEM((shard_len, LANES), BF16),
            pltpu.VMEM((kern_count, 2 * per + 2, LANES), F32),
            pltpu.VMEM((kern_count, per, LANES), F32),
            pltpu.VMEM((kern_count, 2 * per + 2, LANES), F32),
            pltpu.VMEM((per + 1, LANES), F32),
            pltpu.VMEM((kern_count, per + 1, LANES), F32),
            pltpu.VMEM((walk_count, chunks, per + 1, LANES), F32),
            pltpu.VMEM((walk_count, dims, walk_len), F32),
            pltpu.VMEM((walk_count, 1, walk_len), jnp.int32),
            pltpu.VMEM((walk_count, capacity, walk_len), BF16),
            dma((kern_count,)), dma((kern_count,)),
            dma((kern_count,)), dma((kern_count,)),
            dma((walk_count, chunks)), dma((walk_count, chunks)),
            dma((walk_count,)), dma((walk_count,)),
            dma((walk_count,)), dma((walk_count,)),
        ],
        compiler_params=pltpu.CompilerParams(collective_id=0, has_side_effects=True),
        name="sums",
    )(walkers, merge_target.reshape(1, walk_len), centers, sigmas, height_row, kernel_live, norm_old)

    bias, force, new_heights, new_centers, new_sigmas, log_norm = pl.pallas_call(
        functools.partial(merge_kernel, groups),
        out_shape=(
            jax.ShapeDtypeStruct((1, walk_len), F32),
            jax.ShapeDtypeStruct((dims, walk_len), F32),
            jax.ShapeDtypeStruct((1, shard_len), F32),
            jax.ShapeDtypeStruct((dims, shard_len), F32),
            jax.ShapeDtypeStruct((dims, shard_len), F32),
            jax.ShapeDtypeStruct((1, 1), F32),
        ),
        in_specs=[VMEM] * 8 + [SMEM, SMEM],
        out_specs=(VMEM,) * 6,
        name="merge",
    )(share, density, packed, packed_slot, packed_density, centers, sigmas, height_row, new_sigma, norm_old)
    return (bias.reshape(walk_len), force, new_heights.reshape(shard_len), new_centers, new_sigmas, log_norm.reshape(1))


def solution(mesh):
    in_specs = (
        P(None, "walk"),
        P(None, "kern"),
        P(None, "kern"),
        P("kern"),
        P("kern"),
        P("walk"),
        P(),
        P(),
    )
    out_specs = (P("walk"), P(None, "walk"), P("kern"), P(None, "kern"), P(None, "kern"), P())
    return jax.shard_map(
        per_device, mesh=mesh, in_specs=in_specs, out_specs=out_specs, check_vma=False
    )
```

time: 32.7 us -> 24.9 us (0.76)
  Pallas kernels: 30.5 us -> 22.7 us
    pallas_call x2 -> x1, Pallas kernels: 26.3 us -> 20.6 us  [per_device(): pl.pallas_call(functools.partial(sums_kernel, kern_count, walk_count, gro...]
    pallas_call x1, Pallas kernels: 4.22 us -> 2.11 us  [per_device(): pl.pallas_call(functools.partial(merge_kernel, groups), out_shape=(jax.Sh...]
where the time goes in v2:
time: 24.9 us; the launch traced here: 24.7 us
  Pallas kernels  22.7 us (91%)
  between operations  1.93 us (8%)
    pallas_call x1, Pallas kernels, per_device(): pl.pallas_call(functools.partial(sums_kernel, kern_count, walk_count, gro...  20.6 us
    pallas_call x1, Pallas kernels, per_device(): pl.pallas_call(functools.partial(merge_kernel, groups), out_shape=(jax.Sh...  2.11 us

profile of v2, /device:TPU:0, one launch (start us, length us, event | category | flops | bytes accessed | tf_op | source)
XLA Modules:
  0.0 24.7 jit_solution(15869363737577236527)
XLA Ops:
  1.9 20.6 %sums.1 = (f32[16,5,128]{2,1,0:T(8,128)}, f32[2,1,1024]{2,1,0:T(1,128)}, f32[2,8,128]{2,1,0:T(8,128)}, f32[2,1,128]{2,1,0:T(1,128)}, f32[2,1,128]{2,1,0:T(1,128)}) custom-call(f32[8,1024]{1,0:T(8,128)} %walkers_ref.1, s32[1,1024]{1,0:T(1,128)} %bitcast.7, f32[8,2048]{1,0:T(8,128)} %centers_ref.3, f32[8,2048]{1,0:T(8,128)} %sigmas_ref.3, f32[1,2048]{1,0:T(1,128)} %bitcast.5, ...), custom_call_target="tpu_custom_call" | custom-call | tf_op jit(solution)/shard_map/sums/pallas_call | solution.py:385
  22.6 2.1 %merge.1 = (f32[1,1024]{1,0:T(1,128)}, f32[8,1024]{1,0:T(8,128)}, f32[1,2048]{1,0:T(1,128)}, f32[8,2048]{1,0:T(8,128)}, f32[8,2048]{1,0:T(8,128)}, /*index=5*/f32[1,1]{1,0:T(1,128)}) custom-call(f32[16,5,128]{2,1,0:T(8,128)} %get-tuple-element.17.share_ref, f32[2,1,1024]{2,1,0:T(1,128)} %get-tuple-element.18.density_ref, ...), custom_call_target="tpu_custom_call" | custom-call | tf_op jit(solution)/shard_map/merge/pallas_call | solution.py:419

commit v3 on v2

--- a/solution.py
+++ b/solution.py
@@ -17,7 +17,8 @@
 F32 = jnp.float32
 BF16 = jnp.bfloat16
 VMEM = pl.BlockSpec(memory_space=pltpu.VMEM)
-SMEM = pl.BlockSpec(memory_space=pltpu.SMEM)
+GRANT = 24 * 1024 * 1024
+HBM = pl.BlockSpec(memory_space=pltpu.HBM)
 
 
 def split(x):
@@ -41,11 +42,28 @@
 
 
 def sums_kernel(kern_count, walk_count, groups, capacity,
-                walkers_ref, target_ref, centers_ref, sigmas_ref, heights_ref, live_ref, norm_ref,
-                share_ref, density_ref, packed_ref, packed_slot_ref, packed_density_ref,
+                walkers_hbm, target_hbm, centers_hbm, sigmas_hbm, heights_hbm, live_hbm, norm_hbm,
+                share_ref, density_ref, packed_ref, packed_slot_ref, packed_density_ref, norm_out_ref,
+                walkers_ref, target_ref, centers_ref, sigmas_ref, heights_ref, live_ref, norm_ref, load_sem,
                 walker_feat, kernel_feat, kernel_mom, sums, own, got, mine, shared, far,
                 far_walkers, far_targets, table,
                 send_a, recv_a, send_b, recv_b, send_c, recv_c, send_w, recv_w, send_t, recv_t):
+    loads = [
+        pltpu.make_async_copy(source, target, load_sem.at[index])
+        for index, (source, target) in enumerate(
+            [
+                (walkers_hbm, walkers_ref),
+                (centers_hbm, centers_ref),
+                (sigmas_hbm, sigmas_ref),
+                (heights_hbm, heights_ref),
+                (live_hbm, live_ref),
+                (norm_hbm, norm_ref),
+                (target_hbm, target_ref),
+            ]
+        )
+    ]
+    for load in loads:
+        load.start()
     dims, walk_len = walkers_ref.shape
     shard_len = centers_ref.shape[1]
     per = dims // groups
@@ -54,7 +72,6 @@
     walk = lax.axis_index("walk")
     my_chunk = me // groups
     my_group = lax.rem(me, groups)
-    norm = norm_ref[0]
 
     def peer(step):
         return lax.rem(me + step, kern_count)
@@ -81,6 +98,10 @@
 
         lax.fori_loop(0, chunks, greet_far, 0)
 
+    for load in loads:
+        load.wait()
+    norm = norm_ref[0]
+    norm_out_ref[...] = jnp.full((1, 1), norm, F32)
     walkers = walkers_ref[...]
     sq_h, sq_m, sq_l = split(walkers * walkers)
     wk_h, wk_m, wk_l = split(walkers)
@@ -88,7 +109,11 @@
     one = jnp.ones((1, walk_len), F32)
     pad = jnp.zeros((LANES - 12 * dims - 8, walk_len), F32)
     stacked = jnp.concatenate(h + m + h + m + l + h + [row_of([one] * 3, walk_len), pad], 0)
-    walker_feat[...] = stacked.T.astype(BF16)
+    stacked = stacked.astype(BF16)
+    width = 2 * LANES
+    quarters = walk_len // width
+    for quarter in range(quarters):
+        walker_feat[quarter] = stacked[:, quarter * width : (quarter + 1) * width]
 
     centers = centers_ref[...]
     sigmas = sigmas_ref[...]
@@ -100,23 +125,21 @@
     con = row_of(split(LOG2E * constant), shard_len)
     h, m, l = [[k_sq[i], k_lin[i]] for i in range(3)]
     pad = jnp.zeros((LANES - 12 * dims - 8, shard_len), F32)
-    kernel_feat[...] = jnp.concatenate(h + h + m + m + h + l + [con, pad], 0).astype(BF16)
+    kernel_feat[...] = jnp.concatenate(h + h + m + m + h + l + [con, pad], 0).T.astype(BF16)
 
     live = live_ref[0]
     alive = (lax.broadcasted_iota(jnp.int32, (8, shard_len), 1) < live).astype(F32)
     mom_a = split(inverse_var * alive)
     mom_c = split(scaled * alive)
-    pad = jnp.zeros((LANES - 6 * dims - 8, shard_len), F32)
+    pad = jnp.zeros((8, shard_len), F32)
     rows = [mom_a[0], mom_c[0], mom_a[1], mom_c[1], mom_a[2], mom_c[2], row_of([alive], shard_len), pad]
-    kernel_mom[...] = jnp.concatenate(rows, 0).T.astype(BF16)
+    kernel_mom[...] = jnp.concatenate(rows, 0).astype(BF16)
 
     live_row = jnp.full((1, LANES), live, jnp.int32).astype(F32)
     for unit in range(kern_count):
         chunk, group = unit // groups, unit % groups
         own[unit] = walkers[group * per : (group + 1) * per, chunk * LANES : (chunk + 1) * LANES]
 
-    width = 2 * LANES
-    quarters = walk_len // width
     units = kern_count // quarters
     block = min(512, shard_len)
 
@@ -129,19 +152,19 @@
 
     def compute(step):
         quarter = lax.rem(me // units + step, quarters)
-        feat = walker_feat[pl.ds(pl.multiple_of(quarter * width, width), width), :]
+        feat = walker_feat[quarter]
         total = None
         for index in range(shard_len // block):
             part = slice(index * block, (index + 1) * block)
-            e = jnp.exp2(jnp.dot(feat, kernel_feat[:, part], preferred_element_type=F32))
+            e = jnp.exp2(jnp.dot(kernel_feat[part, :], feat, preferred_element_type=F32))
             high = e.astype(BF16)
             low = (e - high.astype(F32)).astype(BF16)
-            moms = kernel_mom[part, :]
-            add = jnp.dot(high, moms, preferred_element_type=F32) + jnp.dot(
-                low, moms, preferred_element_type=F32
+            moms = kernel_mom[:, part]
+            add = jnp.dot(moms, high, preferred_element_type=F32) + jnp.dot(
+                moms, low, preferred_element_type=F32
             )
             total = add if total is None else total + add
-        moments = total.T
+        moments = total
         a_sum = moments[0:dims] + moments[2 * dims : 3 * dims] + moments[4 * dims : 5 * dims]
         c_sum = moments[dims : 2 * dims] + moments[3 * dims : 4 * dims] + moments[5 * dims : 6 * dims]
         density = moments[6 * dims : 6 * dims + 1]
@@ -191,6 +214,55 @@
             send(step)
 
     got[me] = sums[me]
+    def wait_a(step, carry):
+        copy_a(peer(step), peer(step)).wait_recv()
+        return carry
+
+    lax.fori_loop(1, kern_count, wait_a, 0)
+    total = got[0]
+    for source in range(1, kern_count):
+        total = total + got[source]
+
+    live_total = total[2 * per + 1 : 2 * per + 2]
+    density = total[2 * per : 2 * per + 1] / live_total
+    grad = (-own[me] * total[0:per] + total[per : 2 * per]) / live_total
+    ratio = density / norm + EPSILON
+    force = -PREFACTOR * grad / (norm * ratio)
+    mine[0:1, :] = density
+    mine[1 : per + 1, :] = force
+
+    def copy_b(target, source):
+        return pltpu.make_async_remote_copy(
+            src_ref=mine, dst_ref=shared.at[source],
+            send_sem=send_b.at[target], recv_sem=recv_b.at[source],
+            device_id=(target, walk), device_id_type=MESH,
+        )
+
+    def copy_c(step, index, chunk, source):
+        return pltpu.make_async_remote_copy(
+            src_ref=mine, dst_ref=far.at[source, chunk],
+            send_sem=send_c.at[step, index], recv_sem=recv_c.at[source, chunk],
+            device_id=(far_kern(index), other(step)), device_id_type=MESH,
+        )
+
+    def start_b(step, carry):
+        copy_b(peer(step), me).start()
+        return carry
+
+    for step in range(1, walk_count):
+        def start_c(index, carry):
+            copy_c(step, lax.rem(my_chunk + index, chunks), my_chunk, walk).start()
+            return carry
+
+        half = chunks // 2
+        lax.fori_loop(half, chunks, start_c, 0)
+        lax.fori_loop(0, half, start_c, 0)
+    lax.fori_loop(kern_count // 2, kern_count, start_b, 0)
+    lax.fori_loop(1, kern_count // 2, start_b, 0)
+
+    shared[me, 0:1, :] = density
+    shared[me, 1 : per + 1, :] = force
+
     far_walkers[walk] = walkers
     far_targets[walk] = target_ref[...]
     for step in range(1, walk_count):
@@ -227,55 +299,6 @@
         at = 3 * dims
         packed_slot_ref[index] = packed[at : at + 1] + packed[at + 1 : at + 2] + packed[at + 2 : at + 3] - 1.0
 
-    def wait_a(step, carry):
-        copy_a(peer(step), peer(step)).wait_recv()
-        return carry
-
-    lax.fori_loop(1, kern_count, wait_a, 0)
-    total = got[0]
-    for source in range(1, kern_count):
-        total = total + got[source]
-
-    live_total = total[2 * per + 1 : 2 * per + 2]
-    density = total[2 * per : 2 * per + 1] / live_total
-    grad = (-own[me] * total[0:per] + total[per : 2 * per]) / live_total
-    ratio = density / norm + EPSILON
-    force = -PREFACTOR * grad / (norm * ratio)
-    mine[0:1, :] = density
-    mine[1 : per + 1, :] = force
-
-    def copy_b(target, source):
-        return pltpu.make_async_remote_copy(
-            src_ref=mine, dst_ref=shared.at[source],
-            send_sem=send_b.at[target], recv_sem=recv_b.at[source],
-            device_id=(target, walk), device_id_type=MESH,
-        )
-
-    def copy_c(step, index, chunk, source):
-        return pltpu.make_async_remote_copy(
-            src_ref=mine, dst_ref=far.at[source, chunk],
-            send_sem=send_c.at[step, index], recv_sem=recv_c.at[source, chunk],
-            device_id=(far_kern(index), other(step)), device_id_type=MESH,
-        )
-
-    def start_b(step, carry):
-        copy_b(peer(step), me).start()
-        return carry
-
-    for step in range(1, walk_count):
-        def start_c(index, carry):
-            copy_c(step, lax.rem(my_chunk + index, chunks), my_chunk, walk).start()
-            return carry
-
-        half = chunks // 2
-        lax.fori_loop(half, chunks, start_c, 0)
-        lax.fori_loop(0, half, start_c, 0)
-    lax.fori_loop(kern_count // 2, kern_count, start_b, 0)
-    lax.fori_loop(1, kern_count // 2, start_b, 0)
-
-    shared[me, 0:1, :] = density
-    shared[me, 1 : per + 1, :] = force
-
     def wait_b(step, carry):
         copy_b(peer(step), peer(step)).wait_recv()
         return carry
@@ -320,7 +343,7 @@
     capacity = packed_ref.shape[2]
     per = dims // groups
     chunks = walk_len // LANES
-    norm = norm_ref[0]
+    norm = norm_ref[...]
 
     def biased(density):
         return PREFACTOR * jnp.log(density / norm + EPSILON)
@@ -354,10 +377,9 @@
     second = sums[dims : 2 * dims] + (sums[3 * dims : 4 * dims] + sums[5 * dims : 6 * dims])
     at = 6 * dims
     gain = sums[at : at + 1] + (sums[at + 1 : at + 2] + sums[at + 2 : at + 3])
-    dim = lax.broadcasted_iota(jnp.int32, (dims, 1), 0)
-    new_sigma = jnp.zeros((dims, 1), F32)
-    for d in range(dims):
-        new_sigma = jnp.where(dim == d, new_sigma_ref[d], new_sigma)
+    row = lax.broadcasted_iota(jnp.int32, (dims, dims), 0)
+    column = lax.broadcasted_iota(jnp.int32, (dims, dims), 1)
+    new_sigma = jnp.sum(jnp.where(row == column, new_sigma_ref[...], 0.0), 1, keepdims=True)
     centers = centers_ref[...]
     sigmas = sigmas_ref[...]
     heights = heights_ref[...]
@@ -382,7 +404,7 @@
     height_row = heights.reshape(1, shard_len)
 
     dma = pltpu.SemaphoreType.DMA
-    share, density, packed, packed_slot, packed_density = pl.pallas_call(
+    share, density, packed, packed_slot, packed_density, norm_row = pl.pallas_call(
         functools.partial(sums_kernel, kern_count, walk_count, groups, capacity),
         out_shape=(
             jax.ShapeDtypeStruct((kern_count, per + 1, LANES), F32),
@@ -390,13 +412,22 @@
             jax.ShapeDtypeStruct((walk_count, dims, capacity), F32),
             jax.ShapeDtypeStruct((walk_count, 1, capacity), F32),
             jax.ShapeDtypeStruct((walk_count, 1, capacity), F32),
+            jax.ShapeDtypeStruct((1, 1), F32),
         ),
-        in_specs=[VMEM] * 5 + [SMEM, SMEM],
-        out_specs=(VMEM,) * 5,
+        in_specs=[HBM] * 7,
+        out_specs=(VMEM,) * 6,
         scratch_shapes=[
-            pltpu.VMEM((walk_len, LANES), BF16),
-            pltpu.VMEM((LANES, shard_len), BF16),
+            pltpu.VMEM((dims, walk_len), F32),
+            pltpu.VMEM((1, walk_len), jnp.int32),
+            pltpu.VMEM((dims, shard_len), F32),
+            pltpu.VMEM((dims, shard_len), F32),
+            pltpu.VMEM((1, shard_len), F32),
+            pltpu.SMEM((1,), jnp.int32),
+            pltpu.SMEM((1,), F32),
+            dma((7,)),
+            pltpu.VMEM((walk_len // (2 * LANES), LANES, 2 * LANES), BF16),
             pltpu.VMEM((shard_len, LANES), BF16),
+            pltpu.VMEM((6 * dims + 16, shard_len), BF16),
             pltpu.VMEM((kern_count, 2 * per + 2, LANES), F32),
             pltpu.VMEM((kern_count, per, LANES), F32),
             pltpu.VMEM((kern_count, 2 * per + 2, LANES), F32),
@@ -426,10 +457,11 @@
             jax.ShapeDtypeStruct((dims, shard_len), F32),
             jax.ShapeDtypeStruct((1, 1), F32),
         ),
-        in_specs=[VMEM] * 8 + [SMEM, SMEM],
+        in_specs=[VMEM] * 10,
         out_specs=(VMEM,) * 6,
+        compiler_params=pltpu.CompilerParams(vmem_limit_bytes=GRANT),
         name="merge",
-    )(share, density, packed, packed_slot, packed_density, centers, sigmas, height_row, new_sigma, norm_old)
+    )(share, density, packed, packed_slot, packed_density, centers, sigmas, height_row, new_sigma.reshape(1, dims), norm_row)
     return (bias.reshape(walk_len), force, new_heights.reshape(shard_len), new_centers, new_sigmas, log_norm.reshape(1))
 
 

time: 24.9 us -> 26.5 us (1.064)
  local copies, waits for them, and re-layouts: 0 us -> 2.89 us
  Pallas kernels: 22.7 us -> 21.3 us
    unnamed x0 -> x18, local copies, waits for them, and re-layouts: none -> 2.89 us
    pallas_call x1, Pallas kernels: 20.6 us -> 19.4 us  [per_device(): pl.pallas_call(functools.partial(sums_kernel, kern_count, walk_count, gro...]
where the time goes in v3:
time: 26.5 us; the launch traced here: 26.2 us
  Pallas kernels  21.3 us (80%)
  local copies, waits for them, and re-layouts  2.89 us (11%)
  between operations  2 us (8%)
    pallas_call x1, Pallas kernels, per_device(): pl.pallas_call(functools.partial(sums_kernel, kern_count, walk_count, gro...  19.4 us
    unnamed x18, local copies, waits for them, and re-layouts  2.89 us
    pallas_call x1, Pallas kernels, per_device(): pl.pallas_call(functools.partial(merge_kernel, groups), out_shape=(jax.Sh...  1.89 us

profile of v3, /device:TPU:0, one launch (start us, length us, event | category | flops | bytes accessed | tf_op | source)
XLA Modules:
  0.0 26.2 jit_solution(14601003335147138127)
XLA Ops:
  1.9 0.0 copy-start
  1.9 0.0 copy-start.1
  1.9 19.4 %sums.1 = (f32[16,5,128]{2,1,0:T(8,128)}, f32[2,1,1024]{2,1,0:T(1,128)}, f32[2,8,128]{2,1,0:T(8,128)}, f32[2,1,128]{2,1,0:T(1,128)}, f32[2,1,128]{2,1,0:T(1,128)}, /*index=5*/f32[1,1]{1,0:T(1,128)}) custom-call(f32[8,1024]{1,0:T(8,128)} %walkers_hbm.1, s32[1,1024]{1,0:T(1,128)} %bitcast.9, f32[8,2048]{1,0:T(8,128)} %centers_ref.1, f32[8,2048]{1,0:T(8,128)} %sigmas_ref.1, ...), custom_call_target="tpu_custom_call" | custom-call | tf_op jit(solution)/shard_map/sums/pallas_call | solution.py:407
  21.3 0.0 copy-start.3
  21.3 0.0 copy-start.7
  21.4 0.0 copy-start.6
  21.4 0.0 copy-start.8
  21.4 0.0 copy-done
  21.4 0.0 copy-done.1
  21.4 0.6 %copy-done.3 = f32[2048]{0:T(1024)S(1)} copy-done((f32[2048]{0:T(1024)S(1)}, f32[2048]{0:T(1024)}, u32[]{:S(2)}) %copy-start.3) | copy-done | bytes 8216
  22.0 0.0 copy-done.7
  22.0 0.0 copy-done.6
  22.0 0.0 copy-done.8
  22.0 0.0 copy-start.2
  22.0 0.8 %copy-done.2 = f32[16,5,128]{2,1,0:T(8,128)S(1)} copy-done((f32[16,5,128]{2,1,0:T(8,128)S(1)}, f32[16,5,128]{2,1,0:T(8,128)}, u32[]{:S(2)}) %copy-start.2) | copy-done | bytes 40984
  22.9 0.0 copy-start.4
  22.9 0.7 %copy-done.4 = f32[2,1,1024]{2,1,0:T(1,128)S(1)} copy-done((f32[2,1,1024]{2,1,0:T(1,128)S(1)}, f32[2,1,1024]{2,1,0:T(1,128)}, u32[]{:S(2)}) %copy-start.4) | copy-done | bytes 8216
  23.6 0.0 copy-start.5
  23.6 0.7 %copy-done.5 = f32[2,8,128]{2,1,0:T(8,128)S(1)} copy-done((f32[2,8,128]{2,1,0:T(8,128)S(1)}, f32[2,8,128]{2,1,0:T(8,128)}, u32[]{:S(2)}) %copy-start.5) | copy-done | bytes 8216
  24.3 1.9 %merge.1 = (f32[1,1024]{1,0:T(1,128)}, f32[8,1024]{1,0:T(8,128)}, f32[1,2048]{1,0:T(1,128)}, f32[8,2048]{1,0:T(8,128)}, f32[8,2048]{1,0:T(8,128)}, /*index=5*/f32[1,1]{1,0:T(1,128)}) custom-call(f32[16,5,128]{2,1,0:T(8,128)S(1)} %copy-done.2, f32[2,1,1024]{2,1,0:T(1,128)S(1)} %copy-done.4, f32[2,8,128]{2,1,0:T(8,128)S(1)} %copy-done.5, ...), custom_call_target="tpu_custom_call" | custom-call | tf_op jit(solution)/shard_map/merge/pallas_call | solution.py:450
Async XLA Ops:
  1.9 19.5 %copy-start = (f32[8,2048]{1,0:T(8,128)S(1)}, f32[8,2048]{1,0:T(8,128)}, u32[]{:S(2)}) copy-start(f32[8,2048]{1,0:T(8,128)} %centers_ref.1) | copy-start | bytes 196612
  1.9 19.5 %copy-start.1 = (f32[8,2048]{1,0:T(8,128)S(1)}, f32[8,2048]{1,0:T(8,128)}, u32[]{:S(2)}) copy-start(f32[8,2048]{1,0:T(8,128)} %sigmas_ref.1) | copy-start | bytes 196612
  21.3 0.7 %copy-start.3 = (f32[2048]{0:T(1024)S(1)}, f32[2048]{0:T(1024)}, u32[]{:S(2)}) copy-start(f32[2048]{0:T(1024)} %param.11) | copy-start | bytes 24580
  21.3 0.7 %copy-start.7 = (f32[2,1,128]{2,1,0:T(1,128)S(1)}, f32[2,1,128]{2,1,0:T(1,128)}, u32[]{:S(2)}) copy-start(f32[2,1,128]{2,1,0:T(1,128)} %get-tuple-element.22.packed_density_ref) | copy-start | bytes 3076
  21.4 0.7 %copy-start.6 = (f32[2,1,128]{2,1,0:T(1,128)S(1)}, f32[2,1,128]{2,1,0:T(1,128)}, u32[]{:S(2)}) copy-start(f32[2,1,128]{2,1,0:T(1,128)} %get-tuple-element.21.packed_slot_ref) | copy-start | bytes 3076
  21.4 0.7 %copy-start.8 = (f32[8]{0:T(128)S(1)}, f32[8]{0:T(128)}, u32[]{:S(2)}) copy-start(f32[8]{0:T(128)} %param.14) | copy-start | bytes 100
  22.0 0.8 %copy-start.2 = (f32[16,5,128]{2,1,0:T(8,128)S(1)}, f32[16,5,128]{2,1,0:T(8,128)}, u32[]{:S(2)}) copy-start(f32[16,5,128]{2,1,0:T(8,128)} %get-tuple-element.18.share_ref) | copy-start | bytes 122884
  22.9 0.7 %copy-start.4 = (f32[2,1,1024]{2,1,0:T(1,128)S(1)}, f32[2,1,1024]{2,1,0:T(1,128)}, u32[]{:S(2)}) copy-start(f32[2,1,1024]{2,1,0:T(1,128)} %get-tuple-element.19.density_ref) | copy-start | bytes 24580
  23.6 0.7 %copy-start.5 = (f32[2,8,128]{2,1,0:T(8,128)S(1)}, f32[2,8,128]{2,1,0:T(8,128)}, u32[]{:S(2)}) copy-start(f32[2,8,128]{2,1,0:T(8,128)} %get-tuple-element.20.packed_ref) | copy-start | bytes 24580

commit v4 on v3

--- a/solution.py
+++ b/solution.py
@@ -17,7 +17,6 @@
 F32 = jnp.float32
 BF16 = jnp.bfloat16
 VMEM = pl.BlockSpec(memory_space=pltpu.VMEM)
-GRANT = 24 * 1024 * 1024
 HBM = pl.BlockSpec(memory_space=pltpu.HBM)
 
 
@@ -459,7 +458,6 @@
         ),
         in_specs=[VMEM] * 10,
         out_specs=(VMEM,) * 6,
-        compiler_params=pltpu.CompilerParams(vmem_limit_bytes=GRANT),
         name="merge",
     )(share, density, packed, packed_slot, packed_density, centers, sigmas, height_row, new_sigma.reshape(1, dims), norm_row)
     return (bias.reshape(walk_len), force, new_heights.reshape(shard_len), new_centers, new_sigmas, log_norm.reshape(1))

time: 26.5 us -> 24.3 us (0.917)
  local copies, waits for them, and re-layouts: 2.89 us -> 0 us
  Pallas kernels: 21.3 us -> 22.2 us
    unnamed x18 -> x0, local copies, waits for them, and re-layouts: 2.89 us -> none
    pallas_call x1, Pallas kernels: 1.89 us -> 2.78 us  [per_device(): pl.pallas_call(functools.partial(merge_kernel, groups), out_shape=(jax.Sh...]
where the time goes in v4:
time: 24.3 us; the launch traced here: 24.1 us
  Pallas kernels  22.2 us (91%)
  between operations  1.93 us (8%)
    pallas_call x1, Pallas kernels, per_device(): pl.pallas_call(functools.partial(sums_kernel, kern_count, walk_count, gro...  19.4 us
    pallas_call x1, Pallas kernels, per_device(): pl.pallas_call(functools.partial(merge_kernel, groups), out_shape=(jax.Sh...  2.78 us

profile of v4, /device:TPU:0, one launch (start us, length us, event | category | flops | bytes accessed | tf_op | source)
XLA Modules:
  0.0 24.1 jit_solution(1707173345865816987)
XLA Ops:
  1.9 19.4 %sums.1 = (f32[16,5,128]{2,1,0:T(8,128)}, f32[2,1,1024]{2,1,0:T(1,128)}, f32[2,8,128]{2,1,0:T(8,128)}, f32[2,1,128]{2,1,0:T(1,128)}, f32[2,1,128]{2,1,0:T(1,128)}, /*index=5*/f32[1,1]{1,0:T(1,128)}) custom-call(f32[8,1024]{1,0:T(8,128)} %walkers_hbm.1, s32[1,1024]{1,0:T(1,128)} %bitcast.8, f32[8,2048]{1,0:T(8,128)} %centers_ref.1, f32[8,2048]{1,0:T(8,128)} %sigmas_ref.1, ...), custom_call_target="tpu_custom_call" | custom-call | tf_op jit(solution)/shard_map/sums/pallas_call | solution.py:406
  21.3 2.8 %merge.1 = (f32[1,1024]{1,0:T(1,128)}, f32[8,1024]{1,0:T(8,128)}, f32[1,2048]{1,0:T(1,128)}, f32[8,2048]{1,0:T(8,128)}, f32[8,2048]{1,0:T(8,128)}, /*index=5*/f32[1,1]{1,0:T(1,128)}) custom-call(f32[16,5,128]{2,1,0:T(8,128)} %get-tuple-element.18.share_ref, f32[2,1,1024]{2,1,0:T(1,128)} %get-tuple-element.19.density_ref, ...), custom_call_target="tpu_custom_call" | custom-call | tf_op jit(solution)/shard_map/merge/pallas_call | solution.py:449
